TPU v7x, 32 devices: a whole 2x2x4 slice. The times are simulated.
32 devices in a mesh: gx: 8 (over y, x, core), gy: 4 (over z).
Axes of the slice: x: 2, y: 2, z: 4, core: 2. Of those that a mesh axis runs over, the one named last changes fastest.
Arguments:
- date_key: int32 [393216], P(('gx', 'gy')), may hold values from 0 to 4095
- store_key: int32 [393216], P(('gx', 'gy')), may hold values from 0 to 65535
- product_key: int32 [393216], P(('gx', 'gy')), may hold values from 0 to 1048575
- revenue: bfloat16 [393216], P(('gx', 'gy')), may hold values from -0.59765625 to 0.59765625
- row_counts: int32 [32], P(('gx', 'gy')), may hold values from 1 to 12288, 245760 in all
- date_years: int32 [512], P('gx'), may hold values from -2147483648 to 2147483646
- date_flags: int32 [128], P('gx'), may hold values from -2147483648 to 2147483646
- store_flags: int32 [2048], P('gx'), may hold values from -2147483648 to 2147483646
- product_flags: int32 [32768], P('gx'), may hold values from -2147483648 to 2147483646
- brand_words: int32 [349568], P('gx'), may hold values from 0 to 1073741823
Outputs:
- revenue_groups: float32 [16, 1024], replicated
Inputs may be any that keep to these rules, and one draw needn't show every extreme that they name: Rows d * 12288 to d * 12288 + row_counts[d] - 1 of the fact arrays are live; the largest count equals 12288. `date_years`: date k's year code is in bits 4 * (k % 8) of word k // 8. `date_flags`: bit k % 32 of word k // 32 is the flag of row k. `store_flags`: bit k % 32 of word k // 32 is the flag of row k. `product_flags`: bit k % 32 of word k // 32 is the flag of row k. `brand_words`: product with shard o and local index l holds its brand code in bits 10 * (l % 3) of word o * 43696 + l // 3; words past a shard's products are unused.
All inputs are finite; a program needn't handle non-finite values. No bound on the sum of `row_counts` on one device may be relied on, other than what follows from the above.
Results may differ from a plain program's by a relative error of at most 0.0003.
Values sent between devices are 32-bit elements; how exact they have to be, the bound alone decides.
A program may use at most 64 MiB of HBM per device.

v0:
```python
import jax
import jax.numpy as jnp
from jax import lax
from jax.sharding import PartitionSpec as P

BRANDS = 1024
YEARS = 16


def pick_bits(packed, position, width_bits):
    per_word = 32 // width_bits
    chosen = packed[position // per_word]
    shifted = jnp.right_shift(chosen, position % per_word * width_bits)
    return jnp.bitwise_and(shifted, (1 << width_bits) - 1)


def shards(
    date_key,
    store_key,
    product_key,
    revenue,
    row_counts,
    date_years,
    date_flags,
    store_flags,
    product_flags,
    brand_words,
):
    flag_shard = product_flags.shape[0]
    brand_shard = brand_words.shape[0]
    prod_shard = flag_shard * 32
    year_words, date_bits, store_bits, product_bits, brand_table = (
        lax.all_gather(date_years, "gx", axis=0, tiled=True),
        lax.all_gather(date_flags, "gx", axis=0, tiled=True),
        lax.all_gather(store_flags, "gx", axis=0, tiled=True),
        lax.all_gather(product_flags, "gx", axis=0, tiled=True),
        lax.all_gather(brand_words, "gx", axis=0, tiled=True),
    )

    def brand_place(owner_idx, word_idx):
        return owner_idx * brand_shard + word_idx

    def flag_place(owner_idx, word_idx):
        return owner_idx * flag_shard + word_idx

    block_rows = min(4096, date_key.shape[0])
    row_count = row_counts[0]
    block_total = (row_count + block_rows - 1) // block_rows
    high_groups = YEARS * BRANDS // 128

    def add_block(block_idx, totals):
        first_row = block_idx * block_rows
        date_block = lax.dynamic_slice_in_dim(date_key, first_row, block_rows, 0)
        store_block = lax.dynamic_slice_in_dim(store_key, first_row, block_rows, 0)
        product_block = lax.dynamic_slice_in_dim(product_key, first_row, block_rows, 0)
        money_block = lax.dynamic_slice_in_dim(revenue, first_row, block_rows, 0)
        live_rows = first_row + lax.iota(jnp.int32, block_rows) < row_count
        year_code = pick_bits(year_words, date_block, 4)
        owner_idx = product_block // prod_shard
        local_idx = product_block % prod_shard
        flag_word = product_bits[flag_place(owner_idx, local_idx // 32)]
        product_pass = jnp.bitwise_and(jnp.right_shift(flag_word, local_idx % 32), 1)
        passed = (
            pick_bits(date_bits, date_block, 1)
            * pick_bits(store_bits, store_block, 1)
            * product_pass
        )
        word_val = brand_table[brand_place(owner_idx, local_idx // 3)]
        brand_code = jnp.bitwise_and(jnp.right_shift(word_val, local_idx % 3 * 10), 1023)
        kept_rows = live_rows & (passed == 1)
        amount = jnp.where(kept_rows, money_block, jnp.zeros_like(money_block))
        high_row = year_code * (BRANDS // 128) + brand_code // 128
        weighted = jnp.where(
            lax.iota(jnp.int32, high_groups)[:, None] == high_row[None, :],
            amount[None, :],
            jnp.zeros((), jnp.bfloat16),
        )
        low_hot = (lax.iota(jnp.int32, 128)[:, None] == (brand_code % 128)[None, :]).astype(
            jnp.bfloat16
        )
        return totals + lax.dot_general(
            weighted, low_hot, (((1,), (1,)), ((), ())), preferred_element_type=jnp.float32
        )

    totals = lax.fori_loop(0, block_total, add_block, jnp.zeros((high_groups, 128), jnp.float32))
    group_sums = totals.reshape(YEARS, BRANDS)
    result = lax.psum(group_sums, ("gx", "gy"))
    return result


def solution(mesh):
    placed = (
        P(("gx", "gy")),
        P(("gx", "gy")),
        P(("gx", "gy")),
        P(("gx", "gy")),
        P(("gx", "gy")),
        P("gx"),
        P("gx"),
        P("gx"),
        P("gx"),
        P("gx"),
    )
    return jax.shard_map(shards, mesh=mesh, in_specs=placed, out_specs=P(), check_vma=False)
```

profile of v0, /device:TPU:1, one launch (start us, length us, event | category | flops | bytes accessed | tf_op | source)
XLA Modules:
  0.0 643.7 jit_solution(12886607325947073091)
XLA Ops:
  6.5 1.3 dynamic-slice
  8.5 0.0 copy-start.7
  8.5 0.0 copy-start.8
  8.5 0.0 copy-start.6
  8.5 0.0 copy-start.5
  8.5 0.0 copy-start.1
  8.5 0.0 copy-start.2
  8.5 0.0 copy-start.3
  8.5 0.1 broadcast.223
  8.6 1.3 dynamic-update-slice.1
  9.9 1.1 copy-done
  11.0 0.0 all-reduce.9.cloned.1.call-update
  11.0 0.0 all-reduce.7.cloned.1.call-start
  13.0 0.2 dynamic-update-slice
  13.3 0.2 dynamic-update-slice.2
  13.5 7.3 %all-reduce.3 = (s32[512]{0:T(512)S(1)}, s32[128]{0:T(128)S(1)}) all-reduce(s32[512]{0:T(512)S(1)} %dynamic-update-slice, s32[128]{0:T(128)S(1)} %dynamic-update-slice.2), channel_id=1, replica_groups=mesh['gx'=8,'gy'=4] {'gx'}, use_global_device_ids=true, to_apply=%add | all-reduce | flops 640 | bytes 5120
  20.8 10.3 %all-gather = s32[8,1,256]{2,1,0:T(1,128)S(1)} all-gather(s32[1,1,256]{2,1,0:T(1,128)S(1)} %bitcast.8), channel_id=1, replica_groups=mesh['gx'=8,'gy'=4] {'gx'}, dimensions={0}, use_global_device_ids=true | all-gather | bytes 9216 | tf_op jit(solution)/shard_map/all_gather | solution.py:35
  31.1 9.0 %all_gather.19 = s32[32768]{0:T(1024)S(1)} all-gather(s32[4096]{0:T(1024)S(1)} %copy-done.5), channel_id=1, replica_groups=mesh['gx'=8,'gy'=4] {'gx'}, dimensions={0}, use_global_device_ids=true | all-gather | bytes 147456 | tf_op jit(solution)/shard_map/all_gather | solution.py:36
  40.1 30.7 %all-reduce.9.cloned.1.call-done = s32[349568]{0:T(1024)} async-done(((s32[349568]{0:T(1024)}), s32[349568]{0:T(1024)}) %all-reduce.9.cloned.1.call-update) | async-done | bytes 1398288
  70.8 147.5 %while.13 = (s32[]{:T(128)}, f32[128,128]{1,0:T(8,128)S(1)}, s32[]{:T(128)}, s32[12288]{0:T(1024)S(1)}, s32[512]{0:T(512)S(1)}, /*index=5*/s32[12288]{0:T(1024)S...) while((s32[]{:T(128)}, f32[128,128]{1,0:T(8,128)S(1)}, ...), condition=%wide.region_1.2_spmd, body=%wide.region_0.1_spmd.sunk | while | flops 136749056 | bytes 860395 | solution.py:85
  70.9 48.5 %gather_fusion.1 = s32[4096]{0:T(1024)S(1)} fusion(s32[349568]{0:T(1024)} %get-tuple-element.421, s32[4096]{0:T(1024)S(1)} %fusion.57), kind=kCustom, calls=%fused_computation.1.clone.1 | custom fusion | bytes 49152 | tf_op jit(solution)/shard_map/while/body/gather | solution.py:68
  119.5 25.9 %gather_fusion = s32[4096]{0:T(1024)S(1)} fusion(s32[512]{0:T(512)S(1)} %get-tuple-element.419, s32[4096]{0:T(1024)S(1)} %fusion.55), kind=kCustom, calls=%fused_computation.clone.1 | custom fusion | bytes 49152 | tf_op jit(solution)/shard_map/while/body/gather | solution.py:12
  145.4 0.1 fusion.58
  145.5 23.0 %gather_fusion.3 = s32[4096]{0:T(1024)S(1)} fusion(s32[2048]{0:T(1024)S(1)} %get-tuple-element.425, s32[4096]{0:T(1024)S(1)} %get-tuple-element.378), kind=kCustom, calls=%fused_computation.3.clone.1 | custom fusion | bytes 49152 | tf_op jit(solution)/shard_map/while/body/gather | solution.py:12
  168.5 23.0 %gather_fusion.2 = s32[4096]{0:T(1024)S(1)} fusion(s32[32768]{0:T(1024)S(1)} %get-tuple-element.426, s32[4096]{0:T(1024)S(1)} %get-tuple-element.377), kind=kCustom, calls=%fused_computation.4.clone.1 | custom fusion | bytes 49152 | tf_op jit(solution)/shard_map/while/body/gather | solution.py:61
  191.6 24.7 %gather_fusion.4 = s32[4096]{0:T(1024)S(1)} fusion(s32[128]{0:T(128)S(1)} %get-tuple-element.423, s32[4096]{0:T(1024)S(1)} %get-tuple-element.379), kind=kCustom, calls=%fused_computation.2.clone.1 | custom fusion | bytes 49152 | tf_op jit(solution)/shard_map/while/body/gather | solution.py:12
  216.3 1.4 fusion.59
  217.7 0.7 fusion.60
  218.3 0.6 reshape.6
  219.0 0.0 all-reduce.7.cloned.1.call-update
  219.0 416.4 %all-reduce.7.cloned.1.call-done = f32[16,1024]{1,0:T(8,128)} async-done(((f32[16,1024]{1,0:T(8,128)}), f32[16,1024]{1,0:T(8,128)}) %all-reduce.7.cloned.1.call-update) | async-done | bytes 65552 | tf_op jit(solution)/shard_map/psum | solution.py:87
  635.4 1.5 copy.23
  (18 shorter events, 0.2 us)
Async XLA Ops:
  6.5 2.1 copy-start.4
  6.5 64.3 %all-reduce.9.cloned.1.call-start = ((), (), s32[]{:S(2)}) async-start(), calls=%async_computation.1 | async-start | bytes 2801664
  8.5 4.6 copy-start.7
  8.5 4.8 copy-start.8
  8.5 12.3 %copy-start.6 = (s32[256]{0:T(256)S(1)}, s32[256]{0:T(256)}, u32[]{:S(2)}) copy-start(s32[256]{0:T(256)} %param.19) | copy-start | bytes 3076
  8.5 22.6 %copy-start.5 = (s32[4096]{0:T(1024)S(1)}, s32[4096]{0:T(1024)}, u32[]{:S(2)}) copy-start(s32[4096]{0:T(1024)} %param.20) | copy-start | bytes 49156
  8.5 62.3 %copy-start.1 = (s32[12288]{0:T(1024)S(1)}, s32[12288]{0:T(1024)}, u32[]{:S(2)}) copy-start(s32[12288]{0:T(1024)} %param.12) | copy-start | bytes 147460
  8.5 62.3 %copy-start.2 = (s32[12288]{0:T(1024)S(1)}, s32[12288]{0:T(1024)}, u32[]{:S(2)}) copy-start(s32[12288]{0:T(1024)} %param.14) | copy-start | bytes 147460
  8.5 62.3 %copy-start.3 = (s32[12288]{0:T(1024)S(1)}, s32[12288]{0:T(1024)}, u32[]{:S(2)}) copy-start(s32[12288]{0:T(1024)} %param.13) | copy-start | bytes 147460
  9.9 1.1 copy-start
  11.0 624.3 %all-reduce.7.cloned.1.call-start = ((), (), s32[]{:S(2)}) async-start(), calls=%async_computation | async-start | bytes 131072 | tf_op jit(solution)/shard_map/psum | solution.py:87
Sparse Core Ops, SparseCore 0:
  11.2 59.5 all-reduce.8
  219.1 416.1 all-reduce.6
where the time goes:
time: 649 us; the launch traced here: 644 us
  waiting for transfers between devices  447 us (69%)
  local copies, waits for them, and re-layouts  152 us (23%)
  blocking collectives  26.6 us (4%)
  between operations  16.1 us (2%)
    psum x1, waiting for transfers between devices, shards(): result = lax.psum(group_sums, ('gx', 'gy'))  416 us
    gather x3, local copies, waits for them, and re-layouts, pick_bits(): chosen = packed[position // per_word]  73.6 us
    gather x1, local copies, waits for them, and re-layouts, add_block(): word_val = brand_table[brand_place(owner_idx, local_idx // 3)]  48.5 us
    unnamed x3, waiting for transfers between devices  30.8 us
    gather x1, local copies, waits for them, and re-layouts, add_block(): flag_word = product_bits[flag_place(owner_idx, local_idx // 32)]  23 us
  transfers between devices with their start and end apart: 2, of which 2 were waited for; matrix products, arithmetic and copies ran while one was open for 0% of the time, Pallas kernels for 0%

commit v1 on v0

--- a/solution.py
+++ b/solution.py
@@ -5,6 +5,11 @@
 
 BRANDS = 1024
 YEARS = 16
+
+
+def add_all(x, axis):
+    parts = lax.all_gather(x, axis)
+    return jnp.sum(parts, axis=0)
 
 
 def pick_bits(packed, position, width_bits):
@@ -84,7 +89,7 @@
 
     totals = lax.fori_loop(0, block_total, add_block, jnp.zeros((high_groups, 128), jnp.float32))
     group_sums = totals.reshape(YEARS, BRANDS)
-    result = lax.psum(group_sums, ("gx", "gy"))
+    result = add_all(group_sums, ("gx", "gy"))
     return result
 
 

time: 649 us -> 587 us (0.904)
  waiting for transfers between devices: 447 us -> 383 us
    psum x1 -> x0, waiting for transfers between devices: 416 us -> none  [shards(): result = lax.psum(group_sums, ('gx', 'gy'))]
    all_gather x0 -> x1, waiting for transfers between devices: none -> 352 us  [add_all(): parts = lax.all_gather(x, axis)]
where the time goes in v1:
time: 587 us; the launch traced here: 581 us
  waiting for transfers between devices  383 us (65%)
  local copies, waits for them, and re-layouts  151 us (26%)
  blocking collectives  26.6 us (5%)
  between operations  16 us (3%)
    all_gather x1, waiting for transfers between devices, add_all(): parts = lax.all_gather(x, axis)  352 us
    gather x3, local copies, waits for them, and re-layouts, pick_bits(): chosen = packed[position // per_word]  73.6 us
    gather x1, local copies, waits for them, and re-layouts, add_block(): word_val = brand_table[brand_place(owner_idx, local_idx // 3)]  48.5 us
    unnamed x3, waiting for transfers between devices  30.8 us
    gather x1, local copies, waits for them, and re-layouts, add_block(): flag_word = product_bits[flag_place(owner_idx, local_idx // 32)]  23 us
  transfers between devices with their start and end apart: 2, of which 2 were waited for; matrix products, arithmetic and copies ran while one was open for 0% of the time, Pallas kernels for 0%

profile of v1, /device:TPU:1, one launch (start us, length us, event | category | flops | bytes accessed | tf_op | source)
XLA Modules:
  0.0 581.3 jit_solution(2953291015754119969)
XLA Ops:
  6.5 0.0 copy-start.3
  6.6 0.0 copy-start.2
  6.6 0.0 all-reduce.6.cloned.1.call-start
  6.6 1.3 dynamic-slice
  8.6 0.1 broadcast.223
  8.7 2.3 dynamic-update-slice.1
  11.0 0.0 copy-start
  11.0 1.1 copy-done
  12.1 0.0 all-reduce.6.cloned.1.call-update
  12.1 0.0 all-gather.3.cloned.1.call-start
  14.0 0.0 copy-done.6
  14.1 0.2 dynamic-update-slice
  14.3 0.2 dynamic-update-slice.2
  14.5 7.3 %all-reduce.3 = (s32[512]{0:T(512)S(1)}, s32[128]{0:T(128)S(1)}) all-reduce(s32[512]{0:T(512)S(1)} %dynamic-update-slice, s32[128]{0:T(128)S(1)} %dynamic-update-slice.2), channel_id=1, replica_groups=mesh['gx'=8,'gy'=4] {'gx'}, use_global_device_ids=true, to_apply=%add | all-reduce | flops 640 | bytes 5120
  21.8 0.0 copy-done.5
  21.8 10.3 %all-gather = s32[8,1,256]{2,1,0:T(1,128)S(1)} all-gather(s32[1,1,256]{2,1,0:T(1,128)S(1)} %bitcast.8), channel_id=1, replica_groups=mesh['gx'=8,'gy'=4] {'gx'}, dimensions={0}, use_global_device_ids=true | all-gather | bytes 9216 | tf_op jit(solution)/shard_map/all_gather | solution.py:40
  32.1 0.0 copy-done.4
  32.1 9.0 %all_gather.22 = s32[32768]{0:T(1024)S(1)} all-gather(s32[4096]{0:T(1024)S(1)} %copy-done.4), channel_id=1, replica_groups=mesh['gx'=8,'gy'=4] {'gx'}, dimensions={0}, use_global_device_ids=true | all-gather | bytes 147456 | tf_op jit(solution)/shard_map/all_gather | solution.py:41
  41.1 30.7 %all-reduce.6.cloned.1.call-done = s32[349568]{0:T(1024)} async-done(((s32[349568]{0:T(1024)}), s32[349568]{0:T(1024)}) %all-reduce.6.cloned.1.call-update) | async-done | bytes 1398288
  71.9 147.5 %while.13 = (s32[]{:T(128)}, f32[128,128]{1,0:T(8,128)S(1)}, s32[]{:T(128)}, s32[12288]{0:T(1024)S(1)}, s32[512]{0:T(512)S(1)}, /*index=5*/s32[12288]{0:T(1024)S...) while((s32[]{:T(128)}, f32[128,128]{1,0:T(8,128)S(1)}, ...), condition=%wide.region_1.2_spmd, body=%wide.region_0.1_spmd.sunk | while | flops 136749056 | bytes 860395 | solution.py:90
  72.0 48.5 %gather_fusion.1 = s32[4096]{0:T(1024)S(1)} fusion(s32[349568]{0:T(1024)} %get-tuple-element.421, s32[4096]{0:T(1024)S(1)} %fusion.57), kind=kCustom, calls=%fused_computation.1.clone.1 | custom fusion | bytes 49152 | tf_op jit(solution)/shard_map/while/body/gather | solution.py:73
  120.5 25.9 %gather_fusion = s32[4096]{0:T(1024)S(1)} fusion(s32[512]{0:T(512)S(1)} %get-tuple-element.419, s32[4096]{0:T(1024)S(1)} %fusion.55), kind=kCustom, calls=%fused_computation.clone.1 | custom fusion | bytes 49152 | tf_op jit(solution)/shard_map/while/body/gather | solution.py:17
  146.4 0.1 fusion.58
  146.5 23.0 %gather_fusion.3 = s32[4096]{0:T(1024)S(1)} fusion(s32[2048]{0:T(1024)S(1)} %get-tuple-element.425, s32[4096]{0:T(1024)S(1)} %get-tuple-element.378), kind=kCustom, calls=%fused_computation.3.clone.1 | custom fusion | bytes 49152 | tf_op jit(solution)/shard_map/while/body/gather | solution.py:17
  169.5 23.0 %gather_fusion.2 = s32[4096]{0:T(1024)S(1)} fusion(s32[32768]{0:T(1024)S(1)} %get-tuple-element.426, s32[4096]{0:T(1024)S(1)} %get-tuple-element.377), kind=kCustom, calls=%fused_computation.4.clone.1 | custom fusion | bytes 49152 | tf_op jit(solution)/shard_map/while/body/gather | solution.py:66
  192.6 24.7 %gather_fusion.4 = s32[4096]{0:T(1024)S(1)} fusion(s32[128]{0:T(128)S(1)} %get-tuple-element.423, s32[4096]{0:T(1024)S(1)} %get-tuple-element.379), kind=kCustom, calls=%fused_computation.2.clone.1 | custom fusion | bytes 49152 | tf_op jit(solution)/shard_map/while/body/gather | solution.py:17
  217.3 1.4 fusion.59
  218.7 0.7 fusion.60
  219.4 0.6 all_gather_reshape.3
  220.0 0.0 all-gather.3.cloned.1.call-update
  220.0 352.1 %all-gather.3.cloned.1.call-done = f32[32,16,1024]{2,1,0:T(8,128)} async-done(((f32[1,16,1024]{2,1,0:T(8,128)}), f32[32,16,1024]{2,1,0:T(8,128)}) %all-gather.3.cloned.1.call-update) | async-done | bytes 2097168 | tf_op jit(solution)/shard_map/all_gather | solution.py:11
  572.1 2.3 reduce_sum.9
  (16 shorter events, 0.2 us)
Async XLA Ops:
  6.5 7.5 %copy-start.6 = (s32[64]{0:T(128)S(1)}, s32[64]{0:T(128)}, u32[]{:S(2)}) copy-start(s32[64]{0:T(128)} %param.17) | copy-start | bytes 772
  6.5 7.8 %copy-start.7 = (s32[16]{0:T(128)S(1)}, s32[16]{0:T(128)}, u32[]{:S(2)}) copy-start(s32[16]{0:T(128)} %param.18) | copy-start | bytes 196
  6.5 15.3 %copy-start.5 = (s32[256]{0:T(256)S(1)}, s32[256]{0:T(256)}, u32[]{:S(2)}) copy-start(s32[256]{0:T(256)} %param.19) | copy-start | bytes 3076
  6.5 25.6 %copy-start.4 = (s32[4096]{0:T(1024)S(1)}, s32[4096]{0:T(1024)}, u32[]{:S(2)}) copy-start(s32[4096]{0:T(1024)} %param.20) | copy-start | bytes 49156
  6.5 65.3 %copy-start.1 = (s32[12288]{0:T(1024)S(1)}, s32[12288]{0:T(1024)}, u32[]{:S(2)}) copy-start(s32[12288]{0:T(1024)} %param.12) | copy-start | bytes 147460
  6.5 65.3 %copy-start.3 = (s32[12288]{0:T(1024)S(1)}, s32[12288]{0:T(1024)}, u32[]{:S(2)}) copy-start(s32[12288]{0:T(1024)} %param.13) | copy-start | bytes 147460
  6.6 65.3 %copy-start.2 = (s32[12288]{0:T(1024)S(1)}, s32[12288]{0:T(1024)}, u32[]{:S(2)}) copy-start(s32[12288]{0:T(1024)} %param.14) | copy-start | bytes 147460
  6.6 65.3 %all-reduce.6.cloned.1.call-start = ((), (), s32[]{:S(2)}) async-start(), calls=%async_computation.1 | async-start | bytes 2801664
  11.0 1.1 copy-start
  12.1 560.1 %all-gather.3.cloned.1.call-start = ((), (), s32[]{:S(2)}) async-start(), calls=%async_computation | async-start | bytes 2162688 | tf_op jit(solution)/shard_map/all_gather | solution.py:11
Sparse Core Ops, SparseCore 0:
  12.2 59.5 all-reduce.5
  220.2 351.9 all-gather.2
